TPU v7x, 32 devices: a whole 2x2x4 slice. The times are simulated.
32 devices in a mesh: shot: 2 (over y), inline: 4 (over z), xline: 2 (over x), depth: 2 (over core).
Axes of the slice: x: 2, y: 2, z: 4, core: 2. Of those that a mesh axis runs over, the one named last changes fastest.
Arguments:
- forward_now: float32 [2, 32, 64, 256], P(None, ('shot', 'inline'), 'xline', 'depth'), parts along dimension 1, may hold values from -6 to 6
- forward_before: float32 [2, 32, 64, 256], P(None, ('shot', 'inline'), 'xline', 'depth'), parts along dimension 1, may hold values from -6 to 6
- adjoint_now: float32 [2, 32, 64, 256], P(None, ('shot', 'inline'), 'xline', 'depth'), parts along dimension 1, may hold values from -6 to 6
- adjoint_before: float32 [2, 32, 64, 256], P(None, ('shot', 'inline'), 'xline', 'depth'), parts along dimension 1, may hold values from -6 to 6
- courant: float32 [16, 64, 256], P('inline', 'xline', 'depth'), may hold values from 0.04 to 0.15
- thomsen_epsilon: float32 [16, 64, 256], P('inline', 'xline', 'depth'), may hold values from 0.2 to 0.4
- thomsen_delta: float32 [16, 64, 256], P('inline', 'xline', 'depth'), may hold values from 0 to 0.2
- tilt_class: int32 [16, 64, 256], P('inline', 'xline', 'depth'), may hold values from 0 to 15
- azimuth_class: int32 [16, 64, 256], P('inline', 'xline', 'depth'), may hold values from 0 to 31
- tilt_table: float32 [16], replicated, may hold values from -3.140625 to 3.140625
- azimuth_table: float32 [32], replicated, may hold values from -3.140625 to 3.140625
- source_cell: int32 [2], P('shot'), parts along dimension 0, may hold values from 0 to 262143
- wavelet: float32 [8], P('shot'), parts along dimension 0, may hold values from -6 to 6
- receiver_cells: int32 [4096], P('shot'), parts along dimension 0, may hold values from 0 to 262143
- receiver_data: float32 [4, 4096], P(None, 'shot'), parts along dimension 1, may hold values from -6 to 6
Outputs:
- forward_fields: float32 [2, 32, 64, 256], P(None, ('shot', 'inline'), 'xline', 'depth'), parts along dimension 1
- adjoint_fields: float32 [2, 32, 64, 256], P(None, ('shot', 'inline'), 'xline', 'depth'), parts along dimension 1
- migrated_image: float32 [32, 64, 256], P(('shot', 'inline'), 'xline', 'depth'), parts along dimension 0
- traces: float32 [4, 4096], P(None, 'shot'), parts along dimension 1
There are 2 independent parts, one for each index of `shot`. A program takes and returns all parts, laid end to end along the dimension named above; an argument that names none is the same for every part. Nothing has to cross between parts.
All inputs are finite; a program needn't handle non-finite values.
Results may differ from a plain program's by a relative error of at most 0.00002.
Values sent between devices are 32-bit elements; how exact they have to be, the bound alone decides.
A program may use at most 128 MiB of HBM per device.

v0:
```python
import jax
import jax.numpy as jnp
from jax import lax
from jax.sharding import PartitionSpec as P

STEPS = 4


def with_halo(value, sides, width):
    for axis, dim in sides:
        size, length = (lax.axis_size(axis), value.shape[dim])
        up = [(i, (i + 1) % size) for i in range(size - 1)]
        down = [(j, i) for i, j in up]
        last = lax.slice_in_dim(value, length - width, length, axis=dim)
        initial = lax.slice_in_dim(value, 0, width, axis=dim)
        before = lax.ppermute(last, axis, up)
        after = lax.ppermute(initial, axis, down)
        value = jnp.concatenate([before, value, after], axis=dim)
    return value


def differences(padded):
    centre = padded[..., 1:-1, 1:-1, 1:-1]
    inline_inline = padded[..., 2:, 1:-1, 1:-1] + padded[..., :-2, 1:-1, 1:-1] - 2.0 * centre
    xline_xline = padded[..., 1:-1, 2:, 1:-1] + padded[..., 1:-1, :-2, 1:-1] - 2.0 * centre
    depth_depth = padded[..., 1:-1, 1:-1, 2:] + padded[..., 1:-1, 1:-1, :-2] - 2.0 * centre
    inline_xline = 0.25 * (
        padded[..., 2:, 2:, 1:-1]
        - padded[..., 2:, :-2, 1:-1]
        - padded[..., :-2, 2:, 1:-1]
        + padded[..., :-2, :-2, 1:-1]
    )
    inline_depth = 0.25 * (
        padded[..., 2:, 1:-1, 2:]
        - padded[..., 2:, 1:-1, :-2]
        - padded[..., :-2, 1:-1, 2:]
        + padded[..., :-2, 1:-1, :-2]
    )
    xline_depth = 0.25 * (
        padded[..., 1:-1, 2:, 2:]
        - padded[..., 1:-1, 2:, :-2]
        - padded[..., 1:-1, :-2, 2:]
        + padded[..., 1:-1, :-2, :-2]
    )
    return (
        centre,
        inline_inline,
        xline_xline,
        depth_depth,
        inline_xline,
        inline_depth,
        xline_depth,
    )


def advance(padded, before, factors):
    centre, inline_inline, xline_xline, depth_depth, inline_xline, inline_depth, xline_depth = (
        differences(padded)
    )
    axial_part = (
        factors[3] * inline_inline
        + factors[4] * xline_xline
        + factors[5] * depth_depth
        + factors[6] * inline_xline
        + factors[7] * inline_depth
        + factors[8] * xline_depth
    )
    plane_part = (inline_inline + xline_xline + depth_depth)[0::2] - axial_part[0::2]
    pressure = (
        2.0 * centre[0::2] - before[0::2] + factors[0] * plane_part + factors[2] * axial_part[1::2]
    )
    auxiliary = (
        2.0 * centre[1::2] - before[1::2] + factors[1] * plane_part + factors[2] * axial_part[1::2]
    )
    return jnp.stack([pressure[0], auxiliary[0], pressure[1], auxiliary[1]])


def lookup(classes, table_rows):
    class_range = jnp.arange(table_rows.shape[1], dtype=jnp.int32)
    matches = classes[None] == class_range[:, None, None, None]
    return [
        jnp.sum(jnp.where(matches, entry_row[:, None, None, None], 0.0), axis=0)
        for entry_row in table_rows
    ]


def coefficients(
    courant, thomsen_epsilon, thomsen_delta, tilt_class, azimuth_class, tilt_table, azimuth_table
):
    tilt_sine, tilt_cosine = lookup(
        tilt_class, jnp.stack([jnp.sin(tilt_table), jnp.cos(tilt_table)])
    )
    azimuth_cosine, azimuth_sine = lookup(
        azimuth_class, jnp.stack([jnp.cos(azimuth_table), jnp.sin(azimuth_table)])
    )
    axis_first = tilt_sine * azimuth_cosine
    axis_second = tilt_sine * azimuth_sine
    return jnp.stack(
        [
            courant * (1.0 + 2.0 * thomsen_epsilon),
            courant * (1.0 + 2.0 * thomsen_delta),
            courant,
            axis_first * axis_first,
            axis_second * axis_second,
            tilt_cosine * tilt_cosine,
            2.0 * axis_first * axis_second,
            2.0 * axis_first * tilt_cosine,
            2.0 * axis_second * tilt_cosine,
        ]
    )


def locate(cells, anchor, extent, layout):
    inline_at = cells // (layout[0] * layout[1]) - anchor[0]
    xline_at = cells // layout[1] % layout[0] - anchor[1]
    depth_at = cells % layout[1] - anchor[2]
    inside = (
        (inline_at >= 0)
        & (inline_at < extent[0])
        & (xline_at >= 0)
        & (xline_at < extent[1])
        & (depth_at >= 0)
        & (depth_at < extent[2])
    )
    volume = extent[0] * extent[1] * extent[2]
    flat_index = jnp.where(
        inside, (inline_at * extent[1] + xline_at) * extent[2] + depth_at, volume
    )
    return (flat_index, inside)


def deposit(values, flat_index, extent):
    volume = extent[0] * extent[1] * extent[2]
    return jnp.zeros((volume + 1,), jnp.float32).at[flat_index].add(values)[:volume].reshape(extent)


def sample(field, flat_index, inside):
    volume = field.size
    picked = field.reshape(-1)[jnp.minimum(flat_index, volume - 1)]
    return jnp.where(inside, picked, 0.0)


def per_device(
    forward_now,
    forward_before,
    adjoint_now,
    adjoint_before,
    courant,
    thomsen_epsilon,
    thomsen_delta,
    tilt_class,
    azimuth_class,
    tilt_table,
    azimuth_table,
    source_cell,
    wavelet,
    receiver_cells,
    receiver_data,
):
    inline_cells, xline_cells, depth_cells = courant.shape
    layout = (xline_cells * lax.axis_size("xline"), depth_cells * lax.axis_size("depth"))
    anchor = (
        lax.axis_index("inline") * inline_cells,
        lax.axis_index("xline") * xline_cells,
        lax.axis_index("depth") * depth_cells,
    )
    own_extent = (inline_cells, xline_cells, depth_cells)
    own_index, own_inside = locate(receiver_cells, anchor, own_extent, layout)
    current = jnp.concatenate([forward_now, adjoint_now])
    previous = jnp.concatenate([forward_before, adjoint_before])
    image_sum = jnp.zeros(own_extent, jnp.float32)
    records = []
    factors = coefficients(
        courant,
        thomsen_epsilon,
        thomsen_delta,
        tilt_class,
        azimuth_class,
        tilt_table,
        azimuth_table,
    )
    for moment in range(STEPS):
        padded = with_halo(current, (("inline", 1), ("xline", 2), ("depth", 3)), 1)
        shifted = (anchor[0] - 0, anchor[1] - 0, anchor[2] - 0)
        source_index, source_inside = locate(source_cell, shifted, own_extent, layout)
        receiver_index, receiver_inside = locate(receiver_cells, shifted, own_extent, layout)
        source_term = deposit(
            jnp.broadcast_to(wavelet[moment], source_cell.shape), source_index, own_extent
        )
        receiver_term = deposit(receiver_data[moment], receiver_index, own_extent)
        updated = advance(padded, previous, factors) + jnp.stack(
            [source_term, source_term, receiver_term, receiver_term]
        )
        image_sum = image_sum + updated[0] * updated[2] + updated[1] * updated[3]
        records.append(sample(updated[0], own_index, own_inside))
        previous, current = (current, updated)
    traces = lax.psum(jnp.stack(records), ("inline", "xline", "depth"))
    return (current[:2], current[2:], image_sum, traces)


def solution(mesh):
    return jax.shard_map(
        per_device,
        mesh=mesh,
        in_specs=(
            P(None, ("shot", "inline"), "xline", "depth"),
            P(None, ("shot", "inline"), "xline", "depth"),
            P(None, ("shot", "inline"), "xline", "depth"),
            P(None, ("shot", "inline"), "xline", "depth"),
            P("inline", "xline", "depth"),
            P("inline", "xline", "depth"),
            P("inline", "xline", "depth"),
            P("inline", "xline", "depth"),
            P("inline", "xline", "depth"),
            P(),
            P(),
            P("shot"),
            P("shot"),
            P("shot"),
            P(None, "shot"),
        ),
        out_specs=(
            P(None, ("shot", "inline"), "xline", "depth"),
            P(None, ("shot", "inline"), "xline", "depth"),
            P(("shot", "inline"), "xline", "depth"),
            P(None, "shot"),
        ),
        check_vma=False,
    )
```

profile of v0, /device:TPU:0, one launch (start us, length us, event | category | flops | bytes accessed | tf_op | source)
XLA Modules:
  0.0 266.8 jit_solution(2049684719237770810)
XLA Ops:
  0.7 1.0 constant_dynamic-update-slice_fusion.1
  1.7 0.9 constant_dynamic-update-slice_fusion
  2.7 1.4 collective-permute-start
  4.1 5.6 %collective-permute-start.1 = (f32[4,1,32,128]{3,2,1,0:T(8,128)S(1)}, f32[4,1,32,128]{3,2,1,0:T(8,128)S(1)}, u32[]{:S(2)}, u32[]{:S(2)}) collective-permute-start(f32[4,1,32,128]{3,2,1,0:T(8,128)S(1)} %get-tuple-element.111), channel_id=1, source_target_pairs={{0,4},{4,8},{8,12},{1,5},{5,9},{9,13},{2,6},{6,10},{10,14},{3,7},{... | collective-permute-start | bytes 196616 | tf_op jit(solution)/shard_map/ppermute | solution.py:16
  9.7 0.9 constant_dynamic-update-slice_fusion.3
  12.9 1.3 collective-permute-start.2
  14.2 4.5 %collective-permute-start.3 = (f32[4,6,1,128]{3,2,1,0:T(1,128)S(1)}, f32[4,6,1,128]{3,2,1,0:T(1,128)S(1)}, u32[]{:S(2)}, u32[]{:S(2)}) collective-permute-start(f32[4,6,1,128]{3,2,1,0:T(1,128)S(1)} %get-tuple-element.97), channel_id=1, source_target_pairs={{0,2},{1,3},{4,6},{5,7},{8,10},{9,11},{12,14},{13,15},{16,18},{17,... | collective-permute-start | bytes 36872 | tf_op jit(solution)/shard_map/ppermute | solution.py:16
  18.8 1.4 select_dynamic-update-slice_fusion.3
  20.2 13.8 %scatter_custom_fusion = f32[16385]{0:T(1024)S(1)} fusion(s32[2048]{0:T(1024)S(1)} %compare_select_fusion.1, f32[2048]{0:T(1024)S(1)} %bitcast.45, f32[]{:T(128)} %constant.257.clone.1), kind=kCustom, calls=%fused_computation.177 | custom fusion | flops 2048 | bytes 65544 | tf_op jit(solution)/shard_map/scatter-add | solution.py:134
  34.6 1.3 collective-permute-start.4
  35.9 3.1 %collective-permute-start.5 = (f32[4,6,34,1]{3,2,1,0:T(8,128)S(1)}, f32[4,6,34,1]{3,2,1,0:T(8,128)S(1)}, u32[]{:S(2)}, u32[]{:S(2)}) collective-permute-start(f32[4,6,34,1]{3,2,1,0:T(8,128)S(1)} %get-tuple-element.74), channel_id=1, source_target_pairs={{0,1},{2,3},{4,5},{6,7},{8,9},{10,11},{12,13},{14,15},{16,17},{18,... | collective-permute-start | bytes 9800 | tf_op jit(solution)/shard_map/ppermute | solution.py:16
  39.1 1.4 collective-permute-done.5
  42.6 1.3 collective-permute-start.6
  43.9 4.6 %collective-permute-start.7 = (f32[4,1,32,128]{3,2,1,0:T(8,128)S(1)}, f32[4,1,32,128]{3,2,1,0:T(8,128)S(1)}, u32[]{:S(2)}, u32[]{:S(2)}) collective-permute-start(f32[4,1,32,128]{3,2,1,0:T(8,128)S(1)} %get-tuple-element.109), channel_id=1, source_target_pairs={{0,4},{4,8},{8,12},{1,5},{5,9},{9,13},{2,6},{6,10},{10,14},{3,7},{... | collective-permute-start | bytes 196616 | tf_op jit(solution)/shard_map/ppermute | solution.py:16
  49.1 1.2 collective-permute-done.7
  50.3 1.3 collective-permute-start.8
  51.6 4.5 %collective-permute-start.9 = (f32[4,6,1,128]{3,2,1,0:T(1,128)S(1)}, f32[4,6,1,128]{3,2,1,0:T(1,128)S(1)}, u32[]{:S(2)}, u32[]{:S(2)}) collective-permute-start(f32[4,6,1,128]{3,2,1,0:T(1,128)S(1)} %get-tuple-element.93), channel_id=1, source_target_pairs={{0,2},{1,3},{4,6},{5,7},{8,10},{9,11},{12,14},{13,15},{16,18},{17,... | collective-permute-start | bytes 36872 | tf_op jit(solution)/shard_map/ppermute | solution.py:16
  56.2 1.5 select_dynamic-update-slice_fusion.2
  57.7 13.8 %scatter_custom_fusion.1 = f32[16385]{0:T(1024)S(1)} fusion(s32[2048]{0:T(1024)S(1)} %compare_select_fusion.1, f32[2048]{0:T(1024)S(1)} %bitcast.44, f32[]{:T(128)} %constant.257.clone.1), kind=kCustom, calls=%fused_computation.175 | custom fusion | flops 2048 | bytes 65544 | tf_op jit(solution)/shard_map/scatter-add | solution.py:134
  72.1 1.3 collective-permute-start.10
  73.4 3.1 %collective-permute-start.11 = (f32[4,6,34,1]{3,2,1,0:T(8,128)S(1)}, f32[4,6,34,1]{3,2,1,0:T(8,128)S(1)}, u32[]{:S(2)}, u32[]{:S(2)}) collective-permute-start(f32[4,6,34,1]{3,2,1,0:T(8,128)S(1)} %get-tuple-element.72), channel_id=1, source_target_pairs={{0,1},{2,3},{4,5},{6,7},{8,9},{10,11},{12,13},{14,15},{16,17},{18,... | collective-permute-start | bytes 9800 | tf_op jit(solution)/shard_map/ppermute | solution.py:16
  76.6 1.4 collective-permute-done.11
  80.1 1.3 collective-permute-start.12
  81.4 5.0 %collective-permute-start.13 = (f32[4,1,32,128]{3,2,1,0:T(8,128)S(1)}, f32[4,1,32,128]{3,2,1,0:T(8,128)S(1)}, u32[]{:S(2)}, u32[]{:S(2)}) collective-permute-start(f32[4,1,32,128]{3,2,1,0:T(8,128)S(1)} %get-tuple-element.107), channel_id=1, source_target_pairs={{0,4},{4,8},{8,12},{1,5},{5,9},{9,13},{2,6},{6,10},{10,14},{3,7},{... | collective-permute-start | bytes 196616 | tf_op jit(solution)/shard_map/ppermute | solution.py:16
  87.1 1.2 collective-permute-done.13
  88.3 1.3 collective-permute-start.14
  89.6 4.5 %collective-permute-start.15 = (f32[4,6,1,128]{3,2,1,0:T(1,128)S(1)}, f32[4,6,1,128]{3,2,1,0:T(1,128)S(1)}, u32[]{:S(2)}, u32[]{:S(2)}) collective-permute-start(f32[4,6,1,128]{3,2,1,0:T(1,128)S(1)} %get-tuple-element.89), channel_id=1, source_target_pairs={{0,2},{1,3},{4,6},{5,7},{8,10},{9,11},{12,14},{13,15},{16,18},{17,... | collective-permute-start | bytes 36872 | tf_op jit(solution)/shard_map/ppermute | solution.py:16
  94.2 1.5 select_dynamic-update-slice_fusion.1
  95.6 13.8 %scatter_custom_fusion.2 = f32[16385]{0:T(1024)S(1)} fusion(s32[2048]{0:T(1024)S(1)} %compare_select_fusion.1, f32[2048]{0:T(1024)S(1)} %bitcast.43, f32[]{:T(128)} %constant.257.clone.1), kind=kCustom, calls=%fused_computation.173 | custom fusion | flops 2048 | bytes 65544 | tf_op jit(solution)/shard_map/scatter-add | solution.py:134
  110.1 1.3 collective-permute-start.16
  111.4 3.3 %collective-permute-start.17 = (f32[4,6,34,1]{3,2,1,0:T(8,128)S(1)}, f32[4,6,34,1]{3,2,1,0:T(8,128)S(1)}, u32[]{:S(2)}, u32[]{:S(2)}) collective-permute-start(f32[4,6,34,1]{3,2,1,0:T(8,128)S(1)} %get-tuple-element.70), channel_id=1, source_target_pairs={{0,1},{2,3},{4,5},{6,7},{8,9},{10,11},{12,13},{14,15},{16,17},{18,... | collective-permute-start | bytes 9800 | tf_op jit(solution)/shard_map/ppermute | solution.py:16
  114.7 1.2 collective-permute-done.17
  118.0 1.3 collective-permute-start.18
  119.3 5.0 %collective-permute-start.19 = (f32[4,1,32,128]{3,2,1,0:T(8,128)S(1)}, f32[4,1,32,128]{3,2,1,0:T(8,128)S(1)}, u32[]{:S(2)}, u32[]{:S(2)}) collective-permute-start(f32[4,1,32,128]{3,2,1,0:T(8,128)S(1)} %get-tuple-element.105), channel_id=1, source_target_pairs={{0,4},{4,8},{8,12},{1,5},{5,9},{9,13},{2,6},{6,10},{10,14},{3,7},{... | collective-permute-start | bytes 196616 | tf_op jit(solution)/shard_map/ppermute | solution.py:16
  125.0 1.2 collective-permute-done.19
  126.2 1.3 collective-permute-start.20
  127.5 4.5 %collective-permute-start.21 = (f32[4,6,1,128]{3,2,1,0:T(1,128)S(1)}, f32[4,6,1,128]{3,2,1,0:T(1,128)S(1)}, u32[]{:S(2)}, u32[]{:S(2)}) collective-permute-start(f32[4,6,1,128]{3,2,1,0:T(1,128)S(1)} %get-tuple-element.85), channel_id=1, source_target_pairs={{0,2},{1,3},{4,6},{5,7},{8,10},{9,11},{12,14},{13,15},{16,18},{17,... | collective-permute-start | bytes 36872 | tf_op jit(solution)/shard_map/ppermute | solution.py:16
  132.1 1.5 select_dynamic-update-slice_fusion
  133.6 13.8 %scatter_custom_fusion.3 = f32[16385]{0:T(1024)S(1)} fusion(s32[2048]{0:T(1024)S(1)} %compare_select_fusion.1, f32[2048]{0:T(1024)S(1)} %bitcast.42, f32[]{:T(128)} %constant.257.clone.1), kind=kCustom, calls=%fused_computation.171 | custom fusion | flops 2048 | bytes 65544 | tf_op jit(solution)/shard_map/scatter-add | solution.py:134
  148.0 1.3 collective-permute-start.22
  149.3 3.1 %collective-permute-start.23 = (f32[4,6,34,1]{3,2,1,0:T(8,128)S(1)}, f32[4,6,34,1]{3,2,1,0:T(8,128)S(1)}, u32[]{:S(2)}, u32[]{:S(2)}) collective-permute-start(f32[4,6,34,1]{3,2,1,0:T(8,128)S(1)} %get-tuple-element.68), channel_id=1, source_target_pairs={{0,1},{2,3},{4,5},{6,7},{8,9},{10,11},{12,13},{14,15},{16,17},{18,... | collective-permute-start | bytes 9800 | tf_op jit(solution)/shard_map/ppermute | solution.py:16
  152.5 1.4 collective-permute-done.23
  155.9 0.8 fusion.76
  157.4 11.8 %gather_fusion = f32[2048]{0:T(1024)S(1)} fusion(f32[16384]{0:T(1024)S(1)} %bitcast.28, s32[2048]{0:T(1024)S(1)} %get-tuple-element.56), kind=kCustom, calls=%fused_computation | custom fusion | bytes 24576 | tf_op jit(solution)/shard_map/gather | solution.py:139
  169.2 11.8 %gather_fusion.2 = f32[2048]{0:T(1024)S(1)} fusion(f32[16384]{0:T(1024)S(1)} %bitcast.27, s32[2048]{0:T(1024)S(1)} %get-tuple-element.56), kind=kCustom, calls=%fused_computation.2 | custom fusion | bytes 24576 | tf_op jit(solution)/shard_map/gather | solution.py:139
  181.0 11.8 %gather_fusion.1 = f32[2048]{0:T(1024)S(1)} fusion(f32[16384]{0:T(1024)S(1)} %bitcast.26, s32[2048]{0:T(1024)S(1)} %get-tuple-element.56), kind=kCustom, calls=%fused_computation.1 | custom fusion | bytes 24576 | tf_op jit(solution)/shard_map/gather | solution.py:139
  192.8 11.8 %gather_fusion.3 = f32[2048]{0:T(1024)S(1)} fusion(f32[16384]{0:T(1024)S(1)} %bitcast.29, s32[2048]{0:T(1024)S(1)} %get-tuple-element.56), kind=kCustom, calls=%fused_computation.3 | custom fusion | bytes 24576 | tf_op jit(solution)/shard_map/gather | solution.py:139
  204.7 62.2 %psum.7 = f32[4,2048]{1,0:T(4,128)} all-reduce(f32[4,2048]{1,0:T(4,128)S(1)} %pad_maximum_fusion.20), channel_id=1, replica_groups=mesh['shot'=2,'inline'=4,'xline'=2,'depth'=2] {'inline','xline','depth'}, use_global_device_ids=true, to_apply=%region_8.9 | all-reduce | flops 8192 | bytes 65536 | tf_op jit(solution)/shard_map/psum | solution.py:197
  (127 shorter events, 14.7 us)
Async XLA Ops:
  0.6 10.0 %copy-start.14 = (f32[16]{0:T(128)S(1)}, f32[16]{0:T(128)}, u32[]{:S(2)}) copy-start(f32[16]{0:T(128)} %param.32) | copy-start | bytes 196
  0.6 10.0 %copy-start.15 = (f32[32]{0:T(128)S(1)}, f32[32]{0:T(128)}, u32[]{:S(2)}) copy-start(f32[32]{0:T(128)} %param.33) | copy-start | bytes 388
  0.7 10.1 %copy-start.12 = (s32[2048]{0:T(1024)S(1)}, s32[2048]{0:T(1024)}, u32[]{:S(2)}) copy-start(s32[2048]{0:T(1024)} %param.36) | copy-start | bytes 24580
  0.7 10.1 %copy-start.11 = (f32[4,2048]{1,0:T(4,128)S(1)}, f32[4,2048]{1,0:T(4,128)}, u32[]{:S(2)}) copy-start(f32[4,2048]{1,0:T(4,128)} %param.37) | copy-start | bytes 98308
  0.7 10.8 %copy-start.7 = (s32[4,32,128]{2,1,0:T(8,128)S(1)}, s32[4,32,128]{2,1,0:T(8,128)}, u32[]{:S(2)}) copy-start(s32[4,32,128]{2,1,0:T(8,128)} %param.30) | copy-start | bytes 196612
  0.7 11.1 %copy-start.8 = (s32[4,32,128]{2,1,0:T(8,128)S(1)}, s32[4,32,128]{2,1,0:T(8,128)}, u32[]{:S(2)}) copy-start(s32[4,32,128]{2,1,0:T(8,128)} %param.31) | copy-start | bytes 196612
  0.7 11.5 %copy-start.1 = (f32[4,32,128]{2,1,0:T(8,128)S(1)}, f32[4,32,128]{2,1,0:T(8,128)}, u32[]{:S(2)}) copy-start(f32[4,32,128]{2,1,0:T(8,128)} %param.27) | copy-start | bytes 196612
  0.7 11.5 %copy-start.9 = (f32[4,32,128]{2,1,0:T(8,128)S(1)}, f32[4,32,128]{2,1,0:T(8,128)}, u32[]{:S(2)}) copy-start(f32[4,32,128]{2,1,0:T(8,128)} %param.28) | copy-start | bytes 196612
  0.7 11.5 %copy-start.10 = (f32[4,32,128]{2,1,0:T(8,128)S(1)}, f32[4,32,128]{2,1,0:T(8,128)}, u32[]{:S(2)}) copy-start(f32[4,32,128]{2,1,0:T(8,128)} %param.29) | copy-start | bytes 196612
  2.7 10.2 %copy-start.6 = (f32[2,4,32,128]{3,2,1,0:T(8,128)S(1)}, f32[2,4,32,128]{3,2,1,0:T(8,128)}, u32[]{:S(2)}) copy-start(f32[2,4,32,128]{3,2,1,0:T(8,128)} %param.26) | copy-start | bytes 393220
  2.7 10.2 %collective-permute-start = (f32[4,1,32,128]{3,2,1,0:T(8,128)S(1)}, f32[4,1,32,128]{3,2,1,0:T(8,128)S(1)}, u32[]{:S(2)}, u32[]{:S(2)}) collective-permute-start(f32[4,1,32,128]{3,2,1,0:T(8,128)S(1)} %get-tuple-element.112), channel_id=1, source_target_pairs={{4,0},{8,4},{12,8},{5,1},{9,5},{13,9},{6,2},{10,6},{14,10},{7,3},{... | collective-permute-start | bytes 196616 | tf_op jit(solution)/shard_map/ppermute | solution.py:17
  4.1 8.8 %collective-permute-start.1 = (f32[4,1,32,128]{3,2,1,0:T(8,128)S(1)}, f32[4,1,32,128]{3,2,1,0:T(8,128)S(1)}, u32[]{:S(2)}, u32[]{:S(2)}) collective-permute-start(f32[4,1,32,128]{3,2,1,0:T(8,128)S(1)} %get-tuple-element.111), channel_id=1, source_target_pairs={{0,4},{4,8},{8,12},{1,5},{5,9},{9,13},{2,6},{6,10},{10,14},{3,7},{... | collective-permute-start | bytes 196616 | tf_op jit(solution)/shard_map/ppermute | solution.py:16
  11.8 7.0 %copy-start.13 = (f32[4]{0:T(128)S(1)}, f32[4]{0:T(128)}, u32[]{:S(2)}) copy-start(f32[4]{0:T(128)} %param.35) | copy-start | bytes 52
  12.9 21.1 %collective-permute-start.2 = (f32[4,6,1,128]{3,2,1,0:T(1,128)S(1)}, f32[4,6,1,128]{3,2,1,0:T(1,128)S(1)}, u32[]{:S(2)}, u32[]{:S(2)}) collective-permute-start(f32[4,6,1,128]{3,2,1,0:T(1,128)S(1)} %get-tuple-element.98), channel_id=1, source_target_pairs={{2,0},{3,1},{6,4},{7,5},{10,8},{11,9},{14,12},{15,13},{18,16},{19,... | collective-permute-start | bytes 36872 | tf_op jit(solution)/shard_map/ppermute | solution.py:17
  14.2 19.8 %collective-permute-start.3 = (f32[4,6,1,128]{3,2,1,0:T(1,128)S(1)}, f32[4,6,1,128]{3,2,1,0:T(1,128)S(1)}, u32[]{:S(2)}, u32[]{:S(2)}) collective-permute-start(f32[4,6,1,128]{3,2,1,0:T(1,128)S(1)} %get-tuple-element.97), channel_id=1, source_target_pairs={{0,2},{1,3},{4,6},{5,7},{8,10},{9,11},{12,14},{13,15},{16,18},{17,... | collective-permute-start | bytes 36872 | tf_op jit(solution)/shard_map/ppermute | solution.py:16
  34.0 0.6 copy-start.3
  34.6 4.5 %collective-permute-start.4 = (f32[4,6,34,1]{3,2,1,0:T(8,128)S(1)}, f32[4,6,34,1]{3,2,1,0:T(8,128)S(1)}, u32[]{:S(2)}, u32[]{:S(2)}) collective-permute-start(f32[4,6,34,1]{3,2,1,0:T(8,128)S(1)} %get-tuple-element.73), channel_id=1, source_target_pairs={{1,0},{3,2},{5,4},{7,6},{9,8},{11,10},{13,12},{15,14},{17,16},{19,... | collective-permute-start | bytes 9800 | tf_op jit(solution)/shard_map/ppermute | solution.py:17
  35.9 4.5 %collective-permute-start.5 = (f32[4,6,34,1]{3,2,1,0:T(8,128)S(1)}, f32[4,6,34,1]{3,2,1,0:T(8,128)S(1)}, u32[]{:S(2)}, u32[]{:S(2)}) collective-permute-start(f32[4,6,34,1]{3,2,1,0:T(8,128)S(1)} %get-tuple-element.74), channel_id=1, source_target_pairs={{0,1},{2,3},{4,5},{6,7},{8,9},{10,11},{12,13},{14,15},{16,17},{18,... | collective-permute-start | bytes 9800 | tf_op jit(solution)/shard_map/ppermute | solution.py:16
  41.7 0.8 slice-start.2
  42.6 6.6 %collective-permute-start.6 = (f32[4,1,32,128]{3,2,1,0:T(8,128)S(1)}, f32[4,1,32,128]{3,2,1,0:T(8,128)S(1)}, u32[]{:S(2)}, u32[]{:S(2)}) collective-permute-start(f32[4,1,32,128]{3,2,1,0:T(8,128)S(1)} %get-tuple-element.110), channel_id=1, source_target_pairs={{4,0},{8,4},{12,8},{5,1},{9,5},{13,9},{6,2},{10,6},{14,10},{7,3},{... | collective-permute-start | bytes 196616 | tf_op jit(solution)/shard_map/ppermute | solution.py:17
  43.9 6.5 %collective-permute-start.7 = (f32[4,1,32,128]{3,2,1,0:T(8,128)S(1)}, f32[4,1,32,128]{3,2,1,0:T(8,128)S(1)}, u32[]{:S(2)}, u32[]{:S(2)}) collective-permute-start(f32[4,1,32,128]{3,2,1,0:T(8,128)S(1)} %get-tuple-element.109), channel_id=1, source_target_pairs={{0,4},{4,8},{8,12},{1,5},{5,9},{9,13},{2,6},{6,10},{10,14},{3,7},{... | collective-permute-start | bytes 196616 | tf_op jit(solution)/shard_map/ppermute | solution.py:16
  50.3 21.2 %collective-permute-start.8 = (f32[4,6,1,128]{3,2,1,0:T(1,128)S(1)}, f32[4,6,1,128]{3,2,1,0:T(1,128)S(1)}, u32[]{:S(2)}, u32[]{:S(2)}) collective-permute-start(f32[4,6,1,128]{3,2,1,0:T(1,128)S(1)} %get-tuple-element.94), channel_id=1, source_target_pairs={{2,0},{3,1},{6,4},{7,5},{10,8},{11,9},{14,12},{15,13},{18,16},{19,... | collective-permute-start | bytes 36872 | tf_op jit(solution)/shard_map/ppermute | solution.py:17
  51.6 19.9 %collective-permute-start.9 = (f32[4,6,1,128]{3,2,1,0:T(1,128)S(1)}, f32[4,6,1,128]{3,2,1,0:T(1,128)S(1)}, u32[]{:S(2)}, u32[]{:S(2)}) collective-permute-start(f32[4,6,1,128]{3,2,1,0:T(1,128)S(1)} %get-tuple-element.93), channel_id=1, source_target_pairs={{0,2},{1,3},{4,6},{5,7},{8,10},{9,11},{12,14},{13,15},{16,18},{17,... | collective-permute-start | bytes 36872 | tf_op jit(solution)/shard_map/ppermute | solution.py:16
  71.5 0.6 copy-start.4
  72.1 4.5 %collective-permute-start.10 = (f32[4,6,34,1]{3,2,1,0:T(8,128)S(1)}, f32[4,6,34,1]{3,2,1,0:T(8,128)S(1)}, u32[]{:S(2)}, u32[]{:S(2)}) collective-permute-start(f32[4,6,34,1]{3,2,1,0:T(8,128)S(1)} %get-tuple-element.71), channel_id=1, source_target_pairs={{1,0},{3,2},{5,4},{7,6},{9,8},{11,10},{13,12},{15,14},{17,16},{19,... | collective-permute-start | bytes 9800 | tf_op jit(solution)/shard_map/ppermute | solution.py:17
  73.4 4.5 %collective-permute-start.11 = (f32[4,6,34,1]{3,2,1,0:T(8,128)S(1)}, f32[4,6,34,1]{3,2,1,0:T(8,128)S(1)}, u32[]{:S(2)}, u32[]{:S(2)}) collective-permute-start(f32[4,6,34,1]{3,2,1,0:T(8,128)S(1)} %get-tuple-element.72), channel_id=1, source_target_pairs={{0,1},{2,3},{4,5},{6,7},{8,9},{10,11},{12,13},{14,15},{16,17},{18,... | collective-permute-start | bytes 9800 | tf_op jit(solution)/shard_map/ppermute | solution.py:16
  79.2 0.8 slice-start.3
  80.1 7.0 %collective-permute-start.12 = (f32[4,1,32,128]{3,2,1,0:T(8,128)S(1)}, f32[4,1,32,128]{3,2,1,0:T(8,128)S(1)}, u32[]{:S(2)}, u32[]{:S(2)}) collective-permute-start(f32[4,1,32,128]{3,2,1,0:T(8,128)S(1)} %get-tuple-element.108), channel_id=1, source_target_pairs={{4,0},{8,4},{12,8},{5,1},{9,5},{13,9},{6,2},{10,6},{14,10},{7,3},{... | collective-permute-start | bytes 196616 | tf_op jit(solution)/shard_map/ppermute | solution.py:17
  81.4 6.9 %collective-permute-start.13 = (f32[4,1,32,128]{3,2,1,0:T(8,128)S(1)}, f32[4,1,32,128]{3,2,1,0:T(8,128)S(1)}, u32[]{:S(2)}, u32[]{:S(2)}) collective-permute-start(f32[4,1,32,128]{3,2,1,0:T(8,128)S(1)} %get-tuple-element.107), channel_id=1, source_target_pairs={{0,4},{4,8},{8,12},{1,5},{5,9},{9,13},{2,6},{6,10},{10,14},{3,7},{... | collective-permute-start | bytes 196616 | tf_op jit(solution)/shard_map/ppermute | solution.py:16
  88.3 21.2 %collective-permute-start.14 = (f32[4,6,1,128]{3,2,1,0:T(1,128)S(1)}, f32[4,6,1,128]{3,2,1,0:T(1,128)S(1)}, u32[]{:S(2)}, u32[]{:S(2)}) collective-permute-start(f32[4,6,1,128]{3,2,1,0:T(1,128)S(1)} %get-tuple-element.90), channel_id=1, source_target_pairs={{2,0},{3,1},{6,4},{7,5},{10,8},{11,9},{14,12},{15,13},{18,16},{19,... | collective-permute-start | bytes 36872 | tf_op jit(solution)/shard_map/ppermute | solution.py:17
  89.6 19.9 %collective-permute-start.15 = (f32[4,6,1,128]{3,2,1,0:T(1,128)S(1)}, f32[4,6,1,128]{3,2,1,0:T(1,128)S(1)}, u32[]{:S(2)}, u32[]{:S(2)}) collective-permute-start(f32[4,6,1,128]{3,2,1,0:T(1,128)S(1)} %get-tuple-element.89), channel_id=1, source_target_pairs={{0,2},{1,3},{4,6},{5,7},{8,10},{9,11},{12,14},{13,15},{16,18},{17,... | collective-permute-start | bytes 36872 | tf_op jit(solution)/shard_map/ppermute | solution.py:16
  109.4 0.6 copy-start.5
  110.1 4.6 %collective-permute-start.16 = (f32[4,6,34,1]{3,2,1,0:T(8,128)S(1)}, f32[4,6,34,1]{3,2,1,0:T(8,128)S(1)}, u32[]{:S(2)}, u32[]{:S(2)}) collective-permute-start(f32[4,6,34,1]{3,2,1,0:T(8,128)S(1)} %get-tuple-element.69), channel_id=1, source_target_pairs={{1,0},{3,2},{5,4},{7,6},{9,8},{11,10},{13,12},{15,14},{17,16},{19,... | collective-permute-start | bytes 9800 | tf_op jit(solution)/shard_map/ppermute | solution.py:17
  111.4 4.5 %collective-permute-start.17 = (f32[4,6,34,1]{3,2,1,0:T(8,128)S(1)}, f32[4,6,34,1]{3,2,1,0:T(8,128)S(1)}, u32[]{:S(2)}, u32[]{:S(2)}) collective-permute-start(f32[4,6,34,1]{3,2,1,0:T(8,128)S(1)} %get-tuple-element.70), channel_id=1, source_target_pairs={{0,1},{2,3},{4,5},{6,7},{8,9},{10,11},{12,13},{14,15},{16,17},{18,... | collective-permute-start | bytes 9800 | tf_op jit(solution)/shard_map/ppermute | solution.py:16
  117.1 0.8 slice-start.4
  118.0 7.0 %collective-permute-start.18 = (f32[4,1,32,128]{3,2,1,0:T(8,128)S(1)}, f32[4,1,32,128]{3,2,1,0:T(8,128)S(1)}, u32[]{:S(2)}, u32[]{:S(2)}) collective-permute-start(f32[4,1,32,128]{3,2,1,0:T(8,128)S(1)} %get-tuple-element.106), channel_id=1, source_target_pairs={{4,0},{8,4},{12,8},{5,1},{9,5},{13,9},{6,2},{10,6},{14,10},{7,3},{... | collective-permute-start | bytes 196616 | tf_op jit(solution)/shard_map/ppermute | solution.py:17
  119.3 6.9 %collective-permute-start.19 = (f32[4,1,32,128]{3,2,1,0:T(8,128)S(1)}, f32[4,1,32,128]{3,2,1,0:T(8,128)S(1)}, u32[]{:S(2)}, u32[]{:S(2)}) collective-permute-start(f32[4,1,32,128]{3,2,1,0:T(8,128)S(1)} %get-tuple-element.105), channel_id=1, source_target_pairs={{0,4},{4,8},{8,12},{1,5},{5,9},{9,13},{2,6},{6,10},{10,14},{3,7},{... | collective-permute-start | bytes 196616 | tf_op jit(solution)/shard_map/ppermute | solution.py:16
  126.2 21.2 %collective-permute-start.20 = (f32[4,6,1,128]{3,2,1,0:T(1,128)S(1)}, f32[4,6,1,128]{3,2,1,0:T(1,128)S(1)}, u32[]{:S(2)}, u32[]{:S(2)}) collective-permute-start(f32[4,6,1,128]{3,2,1,0:T(1,128)S(1)} %get-tuple-element.86), channel_id=1, source_target_pairs={{2,0},{3,1},{6,4},{7,5},{10,8},{11,9},{14,12},{15,13},{18,16},{19,... | collective-permute-start | bytes 36872 | tf_op jit(solution)/shard_map/ppermute | solution.py:17
  127.5 19.9 %collective-permute-start.21 = (f32[4,6,1,128]{3,2,1,0:T(1,128)S(1)}, f32[4,6,1,128]{3,2,1,0:T(1,128)S(1)}, u32[]{:S(2)}, u32[]{:S(2)}) collective-permute-start(f32[4,6,1,128]{3,2,1,0:T(1,128)S(1)} %get-tuple-element.85), channel_id=1, source_target_pairs={{0,2},{1,3},{4,6},{5,7},{8,10},{9,11},{12,14},{13,15},{16,18},{17,... | collective-permute-start | bytes 36872 | tf_op jit(solution)/shard_map/ppermute | solution.py:16
  147.4 0.6 copy-start.2
  148.0 4.5 %collective-permute-start.22 = (f32[4,6,34,1]{3,2,1,0:T(8,128)S(1)}, f32[4,6,34,1]{3,2,1,0:T(8,128)S(1)}, u32[]{:S(2)}, u32[]{:S(2)}) collective-permute-start(f32[4,6,34,1]{3,2,1,0:T(8,128)S(1)} %get-tuple-element.67), channel_id=1, source_target_pairs={{1,0},{3,2},{5,4},{7,6},{9,8},{11,10},{13,12},{15,14},{17,16},{19,... | collective-permute-start | bytes 9800 | tf_op jit(solution)/shard_map/ppermute | solution.py:17
  149.3 4.5 %collective-permute-start.23 = (f32[4,6,34,1]{3,2,1,0:T(8,128)S(1)}, f32[4,6,34,1]{3,2,1,0:T(8,128)S(1)}, u32[]{:S(2)}, u32[]{:S(2)}) collective-permute-start(f32[4,6,34,1]{3,2,1,0:T(8,128)S(1)} %get-tuple-element.68), channel_id=1, source_target_pairs={{0,1},{2,3},{4,5},{6,7},{8,9},{10,11},{12,13},{14,15},{16,17},{18,... | collective-permute-start | bytes 9800 | tf_op jit(solution)/shard_map/ppermute | solution.py:16
  155.0 0.8 slice-start.1
  155.9 1.5 copy-start
  181.0 11.8 %slice-start = ((f32[4,4,32,128]{3,2,1,0:T(8,128)}), f32[1,4,32,128]{3,2,1,0:T(8,128)S(1)}, s32[]{:S(2)}) async-start(f32[4,4,32,128]{3,2,1,0:T(8,128)} %copy-done), calls=%async_computation | async-start | bytes 131072 | tf_op jit(solution)/shard_map/slice | solution.py:194
where the time goes:
time: 268 us; the launch traced here: 267 us
  other arithmetic  68.5 us (26%)
  starting transfers between devices  66.5 us (25%)
  blocking collectives  62.2 us (23%)
  local copies, waits for them, and re-layouts  55.9 us (21%)
  waiting for transfers between devices  10.9 us (4%)
  between operations  2.87 us (1%)
    psum x1, blocking collectives, per_device(): traces = lax.psum(jnp.stack(records), ('inline', 'xline', 'depth'))  62.2 us
    scatter-add x8, other arithmetic, deposit(): jnp.zeros((volume + 1,), jnp.float32).at[flat_index].add(values)[:volume]  61 us
    ppermute x12, starting transfers between devices, with_halo(): before = lax.ppermute(last, axis, up)  50.9 us
    gather x4, local copies, waits for them, and re-layouts, sample(): picked = field.reshape(-1)[jnp.minimum(flat_index, volume - 1)]  47.1 us
    ppermute x12, starting transfers between devices, with_halo(): after = lax.ppermute(initial, axis, down)  15.6 us
    ppermute x12, waiting for transfers between devices, with_halo(): before = lax.ppermute(last, axis, up)  8.83 us
  transfers between devices with their start and end apart: 24, of which 10 were waited for; matrix products, arithmetic and copies ran while one was open for 24% of the time, Pallas kernels for 0%

commit v1 on v0

--- a/solution.py
+++ b/solution.py
@@ -194,7 +194,7 @@
         image_sum = image_sum + updated[0] * updated[2] + updated[1] * updated[3]
         records.append(sample(updated[0], own_index, own_inside))
         previous, current = (current, updated)
-    traces = lax.psum(jnp.stack(records), ("inline", "xline", "depth"))
+    traces = jnp.sum(lax.all_gather(jnp.stack(records), ("inline", "xline", "depth")), axis=0)
     return (current[:2], current[2:], image_sum, traces)
 
 

time: 268 us -> 229 us (0.85)
  blocking collectives: 62.2 us -> 22.7 us
    psum x1 -> x0, blocking collectives: 62.2 us -> none  [per_device(): traces = lax.psum(jnp.stack(records), ('inline', 'xline', 'depth'))]
    all_gather x0 -> x1, blocking collectives: none -> 22.7 us  [per_device(): lax.all_gather(jnp.stack(records), ('inline', 'xline', 'depth'))]
  transfers between devices with their start and end apart: 24 -> 24, of which waited for: 10 -> 10; matrix products, arithmetic and copies ran while one was open for 24% -> 28% of each run, Pallas kernels for 0% -> 0%
where the time goes in v1:
time: 229 us; the launch traced here: 228 us
  other arithmetic  69.2 us (30%)
  starting transfers between devices  66.5 us (29%)
  local copies, waits for them, and re-layouts  55.9 us (24%)
  blocking collectives  22.7 us (10%)
  waiting for transfers between devices  10.9 us (5%)
  between operations  2.87 us (1%)
    scatter-add x8, other arithmetic, deposit(): jnp.zeros((volume + 1,), jnp.float32).at[flat_index].add(values)[:volume]  61 us
    ppermute x12, starting transfers between devices, with_halo(): before = lax.ppermute(last, axis, up)  50.9 us
    gather x4, local copies, waits for them, and re-layouts, sample(): picked = field.reshape(-1)[jnp.minimum(flat_index, volume - 1)]  47.1 us
    all_gather x1, blocking collectives, per_device(): lax.all_gather(jnp.stack(records), ('inline', 'xline', 'depth'))  22.7 us
    ppermute x12, starting transfers between devices, with_halo(): after = lax.ppermute(initial, axis, down)  15.6 us
    ppermute x12, waiting for transfers between devices, with_halo(): before = lax.ppermute(last, axis, up)  8.83 us
  transfers between devices with their start and end apart: 24, of which 10 were waited for; matrix products, arithmetic and copies ran while one was open for 28% of the time, Pallas kernels for 0%

profile of v1, /device:TPU:0, one launch (start us, length us, event | category | flops | bytes accessed | tf_op | source)
XLA Modules:
  0.0 228.1 jit_solution(12840259031890699644)
XLA Ops:
  0.7 1.0 constant_dynamic-update-slice_fusion.1
  1.7 0.9 constant_dynamic-update-slice_fusion
  2.7 1.4 collective-permute-start
  4.1 5.6 %collective-permute-start.1 = (f32[4,1,32,128]{3,2,1,0:T(8,128)S(1)}, f32[4,1,32,128]{3,2,1,0:T(8,128)S(1)}, u32[]{:S(2)}, u32[]{:S(2)}) collective-permute-start(f32[4,1,32,128]{3,2,1,0:T(8,128)S(1)} %get-tuple-element.111), channel_id=1, source_target_pairs={{0,4},{4,8},{8,12},{1,5},{5,9},{9,13},{2,6},{6,10},{10,14},{3,7},{... | collective-permute-start | bytes 196616 | tf_op jit(solution)/shard_map/ppermute | solution.py:16
  9.7 0.9 constant_dynamic-update-slice_fusion.3
  12.9 1.3 collective-permute-start.2
  14.2 4.5 %collective-permute-start.3 = (f32[4,6,1,128]{3,2,1,0:T(1,128)S(1)}, f32[4,6,1,128]{3,2,1,0:T(1,128)S(1)}, u32[]{:S(2)}, u32[]{:S(2)}) collective-permute-start(f32[4,6,1,128]{3,2,1,0:T(1,128)S(1)} %get-tuple-element.97), channel_id=1, source_target_pairs={{0,2},{1,3},{4,6},{5,7},{8,10},{9,11},{12,14},{13,15},{16,18},{17,... | collective-permute-start | bytes 36872 | tf_op jit(solution)/shard_map/ppermute | solution.py:16
  18.8 1.4 select_dynamic-update-slice_fusion.3
  20.2 13.8 %scatter_custom_fusion = f32[16385]{0:T(1024)S(1)} fusion(s32[2048]{0:T(1024)S(1)} %compare_select_fusion.1, f32[2048]{0:T(1024)S(1)} %bitcast.47, f32[]{:T(128)} %constant.257.clone.1), kind=kCustom, calls=%fused_computation.177 | custom fusion | flops 2048 | bytes 65544 | tf_op jit(solution)/shard_map/scatter-add | solution.py:134
  34.6 1.3 collective-permute-start.4
  35.9 3.1 %collective-permute-start.5 = (f32[4,6,34,1]{3,2,1,0:T(8,128)S(1)}, f32[4,6,34,1]{3,2,1,0:T(8,128)S(1)}, u32[]{:S(2)}, u32[]{:S(2)}) collective-permute-start(f32[4,6,34,1]{3,2,1,0:T(8,128)S(1)} %get-tuple-element.74), channel_id=1, source_target_pairs={{0,1},{2,3},{4,5},{6,7},{8,9},{10,11},{12,13},{14,15},{16,17},{18,... | collective-permute-start | bytes 9800 | tf_op jit(solution)/shard_map/ppermute | solution.py:16
  39.1 1.4 collective-permute-done.5
  42.6 1.3 collective-permute-start.6
  43.9 4.6 %collective-permute-start.7 = (f32[4,1,32,128]{3,2,1,0:T(8,128)S(1)}, f32[4,1,32,128]{3,2,1,0:T(8,128)S(1)}, u32[]{:S(2)}, u32[]{:S(2)}) collective-permute-start(f32[4,1,32,128]{3,2,1,0:T(8,128)S(1)} %get-tuple-element.109), channel_id=1, source_target_pairs={{0,4},{4,8},{8,12},{1,5},{5,9},{9,13},{2,6},{6,10},{10,14},{3,7},{... | collective-permute-start | bytes 196616 | tf_op jit(solution)/shard_map/ppermute | solution.py:16
  49.1 1.2 collective-permute-done.7
  50.3 1.3 collective-permute-start.8
  51.6 4.5 %collective-permute-start.9 = (f32[4,6,1,128]{3,2,1,0:T(1,128)S(1)}, f32[4,6,1,128]{3,2,1,0:T(1,128)S(1)}, u32[]{:S(2)}, u32[]{:S(2)}) collective-permute-start(f32[4,6,1,128]{3,2,1,0:T(1,128)S(1)} %get-tuple-element.93), channel_id=1, source_target_pairs={{0,2},{1,3},{4,6},{5,7},{8,10},{9,11},{12,14},{13,15},{16,18},{17,... | collective-permute-start | bytes 36872 | tf_op jit(solution)/shard_map/ppermute | solution.py:16
  56.2 1.5 select_dynamic-update-slice_fusion.2
  57.7 13.8 %scatter_custom_fusion.1 = f32[16385]{0:T(1024)S(1)} fusion(s32[2048]{0:T(1024)S(1)} %compare_select_fusion.1, f32[2048]{0:T(1024)S(1)} %bitcast.46, f32[]{:T(128)} %constant.257.clone.1), kind=kCustom, calls=%fused_computation.175 | custom fusion | flops 2048 | bytes 65544 | tf_op jit(solution)/shard_map/scatter-add | solution.py:134
  72.1 1.3 collective-permute-start.10
  73.4 3.1 %collective-permute-start.11 = (f32[4,6,34,1]{3,2,1,0:T(8,128)S(1)}, f32[4,6,34,1]{3,2,1,0:T(8,128)S(1)}, u32[]{:S(2)}, u32[]{:S(2)}) collective-permute-start(f32[4,6,34,1]{3,2,1,0:T(8,128)S(1)} %get-tuple-element.72), channel_id=1, source_target_pairs={{0,1},{2,3},{4,5},{6,7},{8,9},{10,11},{12,13},{14,15},{16,17},{18,... | collective-permute-start | bytes 9800 | tf_op jit(solution)/shard_map/ppermute | solution.py:16
  76.6 1.4 collective-permute-done.11
  80.1 1.3 collective-permute-start.12
  81.4 5.0 %collective-permute-start.13 = (f32[4,1,32,128]{3,2,1,0:T(8,128)S(1)}, f32[4,1,32,128]{3,2,1,0:T(8,128)S(1)}, u32[]{:S(2)}, u32[]{:S(2)}) collective-permute-start(f32[4,1,32,128]{3,2,1,0:T(8,128)S(1)} %get-tuple-element.107), channel_id=1, source_target_pairs={{0,4},{4,8},{8,12},{1,5},{5,9},{9,13},{2,6},{6,10},{10,14},{3,7},{... | collective-permute-start | bytes 196616 | tf_op jit(solution)/shard_map/ppermute | solution.py:16
  87.1 1.2 collective-permute-done.13
  88.3 1.3 collective-permute-start.14
  89.6 4.5 %collective-permute-start.15 = (f32[4,6,1,128]{3,2,1,0:T(1,128)S(1)}, f32[4,6,1,128]{3,2,1,0:T(1,128)S(1)}, u32[]{:S(2)}, u32[]{:S(2)}) collective-permute-start(f32[4,6,1,128]{3,2,1,0:T(1,128)S(1)} %get-tuple-element.89), channel_id=1, source_target_pairs={{0,2},{1,3},{4,6},{5,7},{8,10},{9,11},{12,14},{13,15},{16,18},{17,... | collective-permute-start | bytes 36872 | tf_op jit(solution)/shard_map/ppermute | solution.py:16
  94.2 1.5 select_dynamic-update-slice_fusion.1
  95.6 13.8 %scatter_custom_fusion.2 = f32[16385]{0:T(1024)S(1)} fusion(s32[2048]{0:T(1024)S(1)} %compare_select_fusion.1, f32[2048]{0:T(1024)S(1)} %bitcast.45, f32[]{:T(128)} %constant.257.clone.1), kind=kCustom, calls=%fused_computation.173 | custom fusion | flops 2048 | bytes 65544 | tf_op jit(solution)/shard_map/scatter-add | solution.py:134
  110.1 1.3 collective-permute-start.16
  111.4 3.3 %collective-permute-start.17 = (f32[4,6,34,1]{3,2,1,0:T(8,128)S(1)}, f32[4,6,34,1]{3,2,1,0:T(8,128)S(1)}, u32[]{:S(2)}, u32[]{:S(2)}) collective-permute-start(f32[4,6,34,1]{3,2,1,0:T(8,128)S(1)} %get-tuple-element.70), channel_id=1, source_target_pairs={{0,1},{2,3},{4,5},{6,7},{8,9},{10,11},{12,13},{14,15},{16,17},{18,... | collective-permute-start | bytes 9800 | tf_op jit(solution)/shard_map/ppermute | solution.py:16
  114.7 1.2 collective-permute-done.17
  118.0 1.3 collective-permute-start.18
  119.3 5.0 %collective-permute-start.19 = (f32[4,1,32,128]{3,2,1,0:T(8,128)S(1)}, f32[4,1,32,128]{3,2,1,0:T(8,128)S(1)}, u32[]{:S(2)}, u32[]{:S(2)}) collective-permute-start(f32[4,1,32,128]{3,2,1,0:T(8,128)S(1)} %get-tuple-element.105), channel_id=1, source_target_pairs={{0,4},{4,8},{8,12},{1,5},{5,9},{9,13},{2,6},{6,10},{10,14},{3,7},{... | collective-permute-start | bytes 196616 | tf_op jit(solution)/shard_map/ppermute | solution.py:16
  125.0 1.2 collective-permute-done.19
  126.2 1.3 collective-permute-start.20
  127.5 4.5 %collective-permute-start.21 = (f32[4,6,1,128]{3,2,1,0:T(1,128)S(1)}, f32[4,6,1,128]{3,2,1,0:T(1,128)S(1)}, u32[]{:S(2)}, u32[]{:S(2)}) collective-permute-start(f32[4,6,1,128]{3,2,1,0:T(1,128)S(1)} %get-tuple-element.85), channel_id=1, source_target_pairs={{0,2},{1,3},{4,6},{5,7},{8,10},{9,11},{12,14},{13,15},{16,18},{17,... | collective-permute-start | bytes 36872 | tf_op jit(solution)/shard_map/ppermute | solution.py:16
  132.1 1.5 select_dynamic-update-slice_fusion
  133.6 13.8 %scatter_custom_fusion.3 = f32[16385]{0:T(1024)S(1)} fusion(s32[2048]{0:T(1024)S(1)} %compare_select_fusion.1, f32[2048]{0:T(1024)S(1)} %bitcast.44, f32[]{:T(128)} %constant.257.clone.1), kind=kCustom, calls=%fused_computation.171 | custom fusion | flops 2048 | bytes 65544 | tf_op jit(solution)/shard_map/scatter-add | solution.py:134
  148.0 1.3 collective-permute-start.22
  149.3 3.1 %collective-permute-start.23 = (f32[4,6,34,1]{3,2,1,0:T(8,128)S(1)}, f32[4,6,34,1]{3,2,1,0:T(8,128)S(1)}, u32[]{:S(2)}, u32[]{:S(2)}) collective-permute-start(f32[4,6,34,1]{3,2,1,0:T(8,128)S(1)} %get-tuple-element.68), channel_id=1, source_target_pairs={{0,1},{2,3},{4,5},{6,7},{8,9},{10,11},{12,13},{14,15},{16,17},{18,... | collective-permute-start | bytes 9800 | tf_op jit(solution)/shard_map/ppermute | solution.py:16
  152.5 1.4 collective-permute-done.23
  155.9 0.8 fusion.76
  157.4 11.8 %gather_fusion = f32[2048]{0:T(1024)S(1)} fusion(f32[16384]{0:T(1024)S(1)} %bitcast.30, s32[2048]{0:T(1024)S(1)} %get-tuple-element.56), kind=kCustom, calls=%fused_computation | custom fusion | bytes 24576 | tf_op jit(solution)/shard_map/gather | solution.py:139
  169.2 11.8 %gather_fusion.2 = f32[2048]{0:T(1024)S(1)} fusion(f32[16384]{0:T(1024)S(1)} %bitcast.29, s32[2048]{0:T(1024)S(1)} %get-tuple-element.56), kind=kCustom, calls=%fused_computation.2 | custom fusion | bytes 24576 | tf_op jit(solution)/shard_map/gather | solution.py:139
  181.0 11.8 %gather_fusion.1 = f32[2048]{0:T(1024)S(1)} fusion(f32[16384]{0:T(1024)S(1)} %bitcast.28, s32[2048]{0:T(1024)S(1)} %get-tuple-element.56), kind=kCustom, calls=%fused_computation.1 | custom fusion | bytes 24576 | tf_op jit(solution)/shard_map/gather | solution.py:139
  192.8 11.8 %gather_fusion.3 = f32[2048]{0:T(1024)S(1)} fusion(f32[16384]{0:T(1024)S(1)} %bitcast.31, s32[2048]{0:T(1024)S(1)} %get-tuple-element.56), kind=kCustom, calls=%fused_computation.3 | custom fusion | bytes 24576 | tf_op jit(solution)/shard_map/gather | solution.py:139
  204.7 22.7 %all-gather.1 = f32[16,4,2048]{2,1,0:T(4,128)S(1)} all-gather(f32[1,4,2048]{2,1,0:T(4,128)S(1)} %maximum_bitcast_fusion), channel_id=2, replica_groups=mesh['shot'=2,'inline'=4,'xline'=2,'depth'=2] {'inline','xline','depth'}, dimensions={0}, use_global_device_ids=true | all-gather | bytes 557056 | tf_op jit(solution)/shard_map/all_gather | solution.py:197
  (128 shorter events, 15.4 us)
Async XLA Ops:
  0.6 10.0 %copy-start.14 = (f32[16]{0:T(128)S(1)}, f32[16]{0:T(128)}, u32[]{:S(2)}) copy-start(f32[16]{0:T(128)} %param.32) | copy-start | bytes 196
  0.6 10.0 %copy-start.15 = (f32[32]{0:T(128)S(1)}, f32[32]{0:T(128)}, u32[]{:S(2)}) copy-start(f32[32]{0:T(128)} %param.33) | copy-start | bytes 388
  0.7 10.1 %copy-start.12 = (s32[2048]{0:T(1024)S(1)}, s32[2048]{0:T(1024)}, u32[]{:S(2)}) copy-start(s32[2048]{0:T(1024)} %param.36) | copy-start | bytes 24580
  0.7 10.1 %copy-start.11 = (f32[4,2048]{1,0:T(4,128)S(1)}, f32[4,2048]{1,0:T(4,128)}, u32[]{:S(2)}) copy-start(f32[4,2048]{1,0:T(4,128)} %param.37) | copy-start | bytes 98308
  0.7 10.8 %copy-start.7 = (s32[4,32,128]{2,1,0:T(8,128)S(1)}, s32[4,32,128]{2,1,0:T(8,128)}, u32[]{:S(2)}) copy-start(s32[4,32,128]{2,1,0:T(8,128)} %param.30) | copy-start | bytes 196612
  0.7 11.1 %copy-start.8 = (s32[4,32,128]{2,1,0:T(8,128)S(1)}, s32[4,32,128]{2,1,0:T(8,128)}, u32[]{:S(2)}) copy-start(s32[4,32,128]{2,1,0:T(8,128)} %param.31) | copy-start | bytes 196612
  0.7 11.5 %copy-start.1 = (f32[4,32,128]{2,1,0:T(8,128)S(1)}, f32[4,32,128]{2,1,0:T(8,128)}, u32[]{:S(2)}) copy-start(f32[4,32,128]{2,1,0:T(8,128)} %param.27) | copy-start | bytes 196612
  0.7 11.5 %copy-start.9 = (f32[4,32,128]{2,1,0:T(8,128)S(1)}, f32[4,32,128]{2,1,0:T(8,128)}, u32[]{:S(2)}) copy-start(f32[4,32,128]{2,1,0:T(8,128)} %param.28) | copy-start | bytes 196612
  0.7 11.5 %copy-start.10 = (f32[4,32,128]{2,1,0:T(8,128)S(1)}, f32[4,32,128]{2,1,0:T(8,128)}, u32[]{:S(2)}) copy-start(f32[4,32,128]{2,1,0:T(8,128)} %param.29) | copy-start | bytes 196612
  2.7 10.2 %copy-start.6 = (f32[2,4,32,128]{3,2,1,0:T(8,128)S(1)}, f32[2,4,32,128]{3,2,1,0:T(8,128)}, u32[]{:S(2)}) copy-start(f32[2,4,32,128]{3,2,1,0:T(8,128)} %param.26) | copy-start | bytes 393220
  2.7 10.2 %collective-permute-start = (f32[4,1,32,128]{3,2,1,0:T(8,128)S(1)}, f32[4,1,32,128]{3,2,1,0:T(8,128)S(1)}, u32[]{:S(2)}, u32[]{:S(2)}) collective-permute-start(f32[4,1,32,128]{3,2,1,0:T(8,128)S(1)} %get-tuple-element.112), channel_id=1, source_target_pairs={{4,0},{8,4},{12,8},{5,1},{9,5},{13,9},{6,2},{10,6},{14,10},{7,3},{... | collective-permute-start | bytes 196616 | tf_op jit(solution)/shard_map/ppermute | solution.py:17
  4.1 8.8 %collective-permute-start.1 = (f32[4,1,32,128]{3,2,1,0:T(8,128)S(1)}, f32[4,1,32,128]{3,2,1,0:T(8,128)S(1)}, u32[]{:S(2)}, u32[]{:S(2)}) collective-permute-start(f32[4,1,32,128]{3,2,1,0:T(8,128)S(1)} %get-tuple-element.111), channel_id=1, source_target_pairs={{0,4},{4,8},{8,12},{1,5},{5,9},{9,13},{2,6},{6,10},{10,14},{3,7},{... | collective-permute-start | bytes 196616 | tf_op jit(solution)/shard_map/ppermute | solution.py:16
  11.8 7.0 %copy-start.13 = (f32[4]{0:T(128)S(1)}, f32[4]{0:T(128)}, u32[]{:S(2)}) copy-start(f32[4]{0:T(128)} %param.35) | copy-start | bytes 52
  12.9 21.1 %collective-permute-start.2 = (f32[4,6,1,128]{3,2,1,0:T(1,128)S(1)}, f32[4,6,1,128]{3,2,1,0:T(1,128)S(1)}, u32[]{:S(2)}, u32[]{:S(2)}) collective-permute-start(f32[4,6,1,128]{3,2,1,0:T(1,128)S(1)} %get-tuple-element.98), channel_id=1, source_target_pairs={{2,0},{3,1},{6,4},{7,5},{10,8},{11,9},{14,12},{15,13},{18,16},{19,... | collective-permute-start | bytes 36872 | tf_op jit(solution)/shard_map/ppermute | solution.py:17
  14.2 19.8 %collective-permute-start.3 = (f32[4,6,1,128]{3,2,1,0:T(1,128)S(1)}, f32[4,6,1,128]{3,2,1,0:T(1,128)S(1)}, u32[]{:S(2)}, u32[]{:S(2)}) collective-permute-start(f32[4,6,1,128]{3,2,1,0:T(1,128)S(1)} %get-tuple-element.97), channel_id=1, source_target_pairs={{0,2},{1,3},{4,6},{5,7},{8,10},{9,11},{12,14},{13,15},{16,18},{17,... | collective-permute-start | bytes 36872 | tf_op jit(solution)/shard_map/ppermute | solution.py:16
  34.0 0.6 copy-start.3
  34.6 4.5 %collective-permute-start.4 = (f32[4,6,34,1]{3,2,1,0:T(8,128)S(1)}, f32[4,6,34,1]{3,2,1,0:T(8,128)S(1)}, u32[]{:S(2)}, u32[]{:S(2)}) collective-permute-start(f32[4,6,34,1]{3,2,1,0:T(8,128)S(1)} %get-tuple-element.73), channel_id=1, source_target_pairs={{1,0},{3,2},{5,4},{7,6},{9,8},{11,10},{13,12},{15,14},{17,16},{19,... | collective-permute-start | bytes 9800 | tf_op jit(solution)/shard_map/ppermute | solution.py:17
  35.9 4.5 %collective-permute-start.5 = (f32[4,6,34,1]{3,2,1,0:T(8,128)S(1)}, f32[4,6,34,1]{3,2,1,0:T(8,128)S(1)}, u32[]{:S(2)}, u32[]{:S(2)}) collective-permute-start(f32[4,6,34,1]{3,2,1,0:T(8,128)S(1)} %get-tuple-element.74), channel_id=1, source_target_pairs={{0,1},{2,3},{4,5},{6,7},{8,9},{10,11},{12,13},{14,15},{16,17},{18,... | collective-permute-start | bytes 9800 | tf_op jit(solution)/shard_map/ppermute | solution.py:16
  41.7 0.8 slice-start.2
  42.6 6.6 %collective-permute-start.6 = (f32[4,1,32,128]{3,2,1,0:T(8,128)S(1)}, f32[4,1,32,128]{3,2,1,0:T(8,128)S(1)}, u32[]{:S(2)}, u32[]{:S(2)}) collective-permute-start(f32[4,1,32,128]{3,2,1,0:T(8,128)S(1)} %get-tuple-element.110), channel_id=1, source_target_pairs={{4,0},{8,4},{12,8},{5,1},{9,5},{13,9},{6,2},{10,6},{14,10},{7,3},{... | collective-permute-start | bytes 196616 | tf_op jit(solution)/shard_map/ppermute | solution.py:17
  43.9 6.5 %collective-permute-start.7 = (f32[4,1,32,128]{3,2,1,0:T(8,128)S(1)}, f32[4,1,32,128]{3,2,1,0:T(8,128)S(1)}, u32[]{:S(2)}, u32[]{:S(2)}) collective-permute-start(f32[4,1,32,128]{3,2,1,0:T(8,128)S(1)} %get-tuple-element.109), channel_id=1, source_target_pairs={{0,4},{4,8},{8,12},{1,5},{5,9},{9,13},{2,6},{6,10},{10,14},{3,7},{... | collective-permute-start | bytes 196616 | tf_op jit(solution)/shard_map/ppermute | solution.py:16
  50.3 21.2 %collective-permute-start.8 = (f32[4,6,1,128]{3,2,1,0:T(1,128)S(1)}, f32[4,6,1,128]{3,2,1,0:T(1,128)S(1)}, u32[]{:S(2)}, u32[]{:S(2)}) collective-permute-start(f32[4,6,1,128]{3,2,1,0:T(1,128)S(1)} %get-tuple-element.94), channel_id=1, source_target_pairs={{2,0},{3,1},{6,4},{7,5},{10,8},{11,9},{14,12},{15,13},{18,16},{19,... | collective-permute-start | bytes 36872 | tf_op jit(solution)/shard_map/ppermute | solution.py:17
  51.6 19.9 %collective-permute-start.9 = (f32[4,6,1,128]{3,2,1,0:T(1,128)S(1)}, f32[4,6,1,128]{3,2,1,0:T(1,128)S(1)}, u32[]{:S(2)}, u32[]{:S(2)}) collective-permute-start(f32[4,6,1,128]{3,2,1,0:T(1,128)S(1)} %get-tuple-element.93), channel_id=1, source_target_pairs={{0,2},{1,3},{4,6},{5,7},{8,10},{9,11},{12,14},{13,15},{16,18},{17,... | collective-permute-start | bytes 36872 | tf_op jit(solution)/shard_map/ppermute | solution.py:16
  71.5 0.6 copy-start.4
  72.1 4.5 %collective-permute-start.10 = (f32[4,6,34,1]{3,2,1,0:T(8,128)S(1)}, f32[4,6,34,1]{3,2,1,0:T(8,128)S(1)}, u32[]{:S(2)}, u32[]{:S(2)}) collective-permute-start(f32[4,6,34,1]{3,2,1,0:T(8,128)S(1)} %get-tuple-element.71), channel_id=1, source_target_pairs={{1,0},{3,2},{5,4},{7,6},{9,8},{11,10},{13,12},{15,14},{17,16},{19,... | collective-permute-start | bytes 9800 | tf_op jit(solution)/shard_map/ppermute | solution.py:17
  73.4 4.5 %collective-permute-start.11 = (f32[4,6,34,1]{3,2,1,0:T(8,128)S(1)}, f32[4,6,34,1]{3,2,1,0:T(8,128)S(1)}, u32[]{:S(2)}, u32[]{:S(2)}) collective-permute-start(f32[4,6,34,1]{3,2,1,0:T(8,128)S(1)} %get-tuple-element.72), channel_id=1, source_target_pairs={{0,1},{2,3},{4,5},{6,7},{8,9},{10,11},{12,13},{14,15},{16,17},{18,... | collective-permute-start | bytes 9800 | tf_op jit(solution)/shard_map/ppermute | solution.py:16
  79.2 0.8 slice-start.3
  80.1 7.0 %collective-permute-start.12 = (f32[4,1,32,128]{3,2,1,0:T(8,128)S(1)}, f32[4,1,32,128]{3,2,1,0:T(8,128)S(1)}, u32[]{:S(2)}, u32[]{:S(2)}) collective-permute-start(f32[4,1,32,128]{3,2,1,0:T(8,128)S(1)} %get-tuple-element.108), channel_id=1, source_target_pairs={{4,0},{8,4},{12,8},{5,1},{9,5},{13,9},{6,2},{10,6},{14,10},{7,3},{... | collective-permute-start | bytes 196616 | tf_op jit(solution)/shard_map/ppermute | solution.py:17
  81.4 6.9 %collective-permute-start.13 = (f32[4,1,32,128]{3,2,1,0:T(8,128)S(1)}, f32[4,1,32,128]{3,2,1,0:T(8,128)S(1)}, u32[]{:S(2)}, u32[]{:S(2)}) collective-permute-start(f32[4,1,32,128]{3,2,1,0:T(8,128)S(1)} %get-tuple-element.107), channel_id=1, source_target_pairs={{0,4},{4,8},{8,12},{1,5},{5,9},{9,13},{2,6},{6,10},{10,14},{3,7},{... | collective-permute-start | bytes 196616 | tf_op jit(solution)/shard_map/ppermute | solution.py:16
  88.3 21.2 %collective-permute-start.14 = (f32[4,6,1,128]{3,2,1,0:T(1,128)S(1)}, f32[4,6,1,128]{3,2,1,0:T(1,128)S(1)}, u32[]{:S(2)}, u32[]{:S(2)}) collective-permute-start(f32[4,6,1,128]{3,2,1,0:T(1,128)S(1)} %get-tuple-element.90), channel_id=1, source_target_pairs={{2,0},{3,1},{6,4},{7,5},{10,8},{11,9},{14,12},{15,13},{18,16},{19,... | collective-permute-start | bytes 36872 | tf_op jit(solution)/shard_map/ppermute | solution.py:17
  89.6 19.9 %collective-permute-start.15 = (f32[4,6,1,128]{3,2,1,0:T(1,128)S(1)}, f32[4,6,1,128]{3,2,1,0:T(1,128)S(1)}, u32[]{:S(2)}, u32[]{:S(2)}) collective-permute-start(f32[4,6,1,128]{3,2,1,0:T(1,128)S(1)} %get-tuple-element.89), channel_id=1, source_target_pairs={{0,2},{1,3},{4,6},{5,7},{8,10},{9,11},{12,14},{13,15},{16,18},{17,... | collective-permute-start | bytes 36872 | tf_op jit(solution)/shard_map/ppermute | solution.py:16
  109.4 0.6 copy-start.5
  110.1 4.6 %collective-permute-start.16 = (f32[4,6,34,1]{3,2,1,0:T(8,128)S(1)}, f32[4,6,34,1]{3,2,1,0:T(8,128)S(1)}, u32[]{:S(2)}, u32[]{:S(2)}) collective-permute-start(f32[4,6,34,1]{3,2,1,0:T(8,128)S(1)} %get-tuple-element.69), channel_id=1, source_target_pairs={{1,0},{3,2},{5,4},{7,6},{9,8},{11,10},{13,12},{15,14},{17,16},{19,... | collective-permute-start | bytes 9800 | tf_op jit(solution)/shard_map/ppermute | solution.py:17
  111.4 4.5 %collective-permute-start.17 = (f32[4,6,34,1]{3,2,1,0:T(8,128)S(1)}, f32[4,6,34,1]{3,2,1,0:T(8,128)S(1)}, u32[]{:S(2)}, u32[]{:S(2)}) collective-permute-start(f32[4,6,34,1]{3,2,1,0:T(8,128)S(1)} %get-tuple-element.70), channel_id=1, source_target_pairs={{0,1},{2,3},{4,5},{6,7},{8,9},{10,11},{12,13},{14,15},{16,17},{18,... | collective-permute-start | bytes 9800 | tf_op jit(solution)/shard_map/ppermute | solution.py:16
  117.1 0.8 slice-start.4
  118.0 7.0 %collective-permute-start.18 = (f32[4,1,32,128]{3,2,1,0:T(8,128)S(1)}, f32[4,1,32,128]{3,2,1,0:T(8,128)S(1)}, u32[]{:S(2)}, u32[]{:S(2)}) collective-permute-start(f32[4,1,32,128]{3,2,1,0:T(8,128)S(1)} %get-tuple-element.106), channel_id=1, source_target_pairs={{4,0},{8,4},{12,8},{5,1},{9,5},{13,9},{6,2},{10,6},{14,10},{7,3},{... | collective-permute-start | bytes 196616 | tf_op jit(solution)/shard_map/ppermute | solution.py:17
  119.3 6.9 %collective-permute-start.19 = (f32[4,1,32,128]{3,2,1,0:T(8,128)S(1)}, f32[4,1,32,128]{3,2,1,0:T(8,128)S(1)}, u32[]{:S(2)}, u32[]{:S(2)}) collective-permute-start(f32[4,1,32,128]{3,2,1,0:T(8,128)S(1)} %get-tuple-element.105), channel_id=1, source_target_pairs={{0,4},{4,8},{8,12},{1,5},{5,9},{9,13},{2,6},{6,10},{10,14},{3,7},{... | collective-permute-start | bytes 196616 | tf_op jit(solution)/shard_map/ppermute | solution.py:16
  126.2 21.2 %collective-permute-start.20 = (f32[4,6,1,128]{3,2,1,0:T(1,128)S(1)}, f32[4,6,1,128]{3,2,1,0:T(1,128)S(1)}, u32[]{:S(2)}, u32[]{:S(2)}) collective-permute-start(f32[4,6,1,128]{3,2,1,0:T(1,128)S(1)} %get-tuple-element.86), channel_id=1, source_target_pairs={{2,0},{3,1},{6,4},{7,5},{10,8},{11,9},{14,12},{15,13},{18,16},{19,... | collective-permute-start | bytes 36872 | tf_op jit(solution)/shard_map/ppermute | solution.py:17
  127.5 19.9 %collective-permute-start.21 = (f32[4,6,1,128]{3,2,1,0:T(1,128)S(1)}, f32[4,6,1,128]{3,2,1,0:T(1,128)S(1)}, u32[]{:S(2)}, u32[]{:S(2)}) collective-permute-start(f32[4,6,1,128]{3,2,1,0:T(1,128)S(1)} %get-tuple-element.85), channel_id=1, source_target_pairs={{0,2},{1,3},{4,6},{5,7},{8,10},{9,11},{12,14},{13,15},{16,18},{17,... | collective-permute-start | bytes 36872 | tf_op jit(solution)/shard_map/ppermute | solution.py:16
  147.4 0.6 copy-start.2
  148.0 4.5 %collective-permute-start.22 = (f32[4,6,34,1]{3,2,1,0:T(8,128)S(1)}, f32[4,6,34,1]{3,2,1,0:T(8,128)S(1)}, u32[]{:S(2)}, u32[]{:S(2)}) collective-permute-start(f32[4,6,34,1]{3,2,1,0:T(8,128)S(1)} %get-tuple-element.67), channel_id=1, source_target_pairs={{1,0},{3,2},{5,4},{7,6},{9,8},{11,10},{13,12},{15,14},{17,16},{19,... | collective-permute-start | bytes 9800 | tf_op jit(solution)/shard_map/ppermute | solution.py:17
  149.3 4.5 %collective-permute-start.23 = (f32[4,6,34,1]{3,2,1,0:T(8,128)S(1)}, f32[4,6,34,1]{3,2,1,0:T(8,128)S(1)}, u32[]{:S(2)}, u32[]{:S(2)}) collective-permute-start(f32[4,6,34,1]{3,2,1,0:T(8,128)S(1)} %get-tuple-element.68), channel_id=1, source_target_pairs={{0,1},{2,3},{4,5},{6,7},{8,9},{10,11},{12,13},{14,15},{16,17},{18,... | collective-permute-start | bytes 9800 | tf_op jit(solution)/shard_map/ppermute | solution.py:16
  155.0 0.8 slice-start.1
  155.9 1.5 copy-start
  181.0 11.8 %slice-start = ((f32[4,4,32,128]{3,2,1,0:T(8,128)}), f32[1,4,32,128]{3,2,1,0:T(8,128)S(1)}, s32[]{:S(2)}) async-start(f32[4,4,32,128]{3,2,1,0:T(8,128)} %copy-done), calls=%async_computation | async-start | bytes 131072 | tf_op jit(solution)/shard_map/slice | solution.py:194
